TPU v7x, 128 devices: a whole 4x4x4 slice. The times are simulated.
128 devices in a mesh: rows: 32 (over z, y, core), cols: 4 (over x).
Axes of the slice: x: 4, y: 4, z: 4, core: 2. Of those that a mesh axis runs over, the one named last changes fastest.
Arguments:
- w_gate: float32 [2048, 8192], P('rows', 'cols'), may hold values from -0.25 to 0.25
- first_gate: float32 [2048, 8192], P('rows', 'cols'), may hold values from -6 to 6
- second_gate: float32 [2048, 8192], P('rows', 'cols'), may hold values from 0.1 to 10
- w_up: float32 [2048, 8192], P('rows', 'cols'), may hold values from -0.25 to 0.25
- first_up: float32 [2048, 8192], P('rows', 'cols'), may hold values from -6 to 6
- second_up: float32 [2048, 8192], P('rows', 'cols'), may hold values from 0.1 to 10
- norm_train: float32 [2048], P(('rows', 'cols')), may hold values from 0.25 to 1.75
- norm_step: float32 [2048], P(('rows', 'cols')), may hold values from -0.3 to 0.3
Outputs:
- ready_gate: bfloat16 [2048, 8192], P(None, 'cols')
- ready_up: bfloat16 [2048, 8192], P(None, 'cols')
- column_gate: float32 [8192], P('cols')
- column_up: float32 [8192], P('cols')
- serve_norm: bfloat16 [2048], replicated
- latest_gate: float32 [2048, 8192], P('rows', 'cols')
- latest_up: float32 [2048, 8192], P('rows', 'cols')
All inputs are finite; a program needn't handle non-finite values. Where the computation divides by a largest or mean magnitude, that divisor is 1e-20 or more.
Results may differ from a plain program's by a relative error of at most 0.001.
Values may be sent and summed in bfloat16 or wider, within the bound.
No kernel may reach another device: no remote copies, remote signals or barrier semaphores. Data moves between devices by JAX's collectives and lax.ppermute only.
A program may use at most 128 MiB of HBM per device.

v0:
```python
import functools
import math
import jax
import jax.numpy as jnp
from jax import lax
from jax.experimental import pallas as pl
from jax.experimental.pallas import tpu as pltpu
from jax.sharding import Mesh
from jax.sharding import PartitionSpec as P

D_MODEL = 2048
ROWS = ("z", "y", "core")
ALL = ("z", "y", "core", "x")

learn_rate = 0.01
decay_rate = 0.1
tiny_value = 1e-08

OCTAVES = 125.5
SLABS = 16
UNROLL = 16
BLOCK = 64 * SLABS + SLABS
VMEM = pl.BlockSpec(memory_space=pltpu.VMEM)
HBM = pl.BlockSpec(memory_space=pltpu.HBM)
READY = jax.ShapeDtypeStruct((D_MODEL, D_MODEL), jnp.bfloat16)

DECODES = {
    "dec_0": (("a", 0), ("a", 1)),
    "dec_1": (("b", 0), ("b", 1)),
    "dec_2": (("c", 0), ("c", 1)),
    "dec_3": (("g1", 0),),
    "dec_4": (("g1", 1), ("g2", 0)),
    "dec_5": (("g2", 1),),
}
HELD = {
    "a": [(o, a, 0) for o in (0, 1) for a in (0, 1, 3)],
    "b": [(o, 0, b) for b in (1, 3) for o in (0, 1)] + [(o, a, b) for b in (1, 3) for o in (0, 1) for a in (1, 3)],
    "c": [(o, 2, b) for b in (0, 1, 3) for o in (0, 1)],
    "g1": [(o, a, 2) for o in (0, 1) for a in (0, 1, 3)],
    "g2": [(o, 2, 2) for o in (0, 1)],
}


def number(z, y, c):
    return (z % 4 * 4 + y % 4) * 2 + c


def near_far(by_near, by_far):
    return [
        (number(z, y, c), number(z + by_far, y + by_near, c) if c == 0 else number(z + by_near, y + by_far, c))
        for z in range(4)
        for y in range(4)
        for c in range(2)
    ]


def near(value, by):
    return lax.ppermute(value, ROWS, near_far(by, 0))


def far(value, by):
    return lax.ppermute(value, ROWS, near_far(0, by))


def swapped(value):
    return lax.ppermute(value, "core", [(0, 1), (1, 0)])


def step_kernel(w_g, f_g, s_g, w_u, f_u, s_u, norm, change, latest_g, latest_u, code, sums, *scratch):
    held, sem, tops, gains = scratch[:6], scratch[6], scratch[7], scratch[8]
    wide = 512
    chunks = D_MODEL // wide
    sources = (w_g, f_g, s_g, w_u, f_u, s_u)
    copies = []
    for k in range(chunks):
        at = pl.ds(k * wide, wide)
        for i in range(6):
            copies.append(pltpu.make_async_copy(sources[i].at[:, at], held[i].at[:, at], sem.at[k * 6 + i]))
    for i, source in enumerate((norm, change)):
        copies.append(pltpu.make_async_copy(source, gains.at[pl.ds(i, 1), :], sem.at[6 * chunks + i]))
    for one in copies:
        one.start()
    for k in range(chunks):
        for o, latest in ((0, latest_g), (1, latest_u)):
            for i in range(3):
                copies[k * 6 + 3 * o + i].wait()
            for slab in range(k * wide // 128, (k + 1) * wide // 128):
                at = pl.ds(slab * 128, 128)
                w, first, second = (held[3 * o + i][:, at] for i in range(3))
                new = w - learn_rate * (first / (jnp.sqrt(second) + tiny_value) + decay_rate * w)
                latest[:, at] = new
                size = jnp.abs(new)
                sums[pl.ds(SLABS * o + slab, 1), :] = jnp.sum(size, axis=0, keepdims=True)
                top = (jnp.max(size, axis=0, keepdims=True) * 1.01).astype(jnp.bfloat16).astype(jnp.float32)
                code[pl.ds(BLOCK * o + 64 * slab, 64), :] = jnp.exp2(new * (OCTAVES / jnp.maximum(top, 1e-35))).astype(
                    jnp.bfloat16
                )
                tops[pl.ds(SLABS * o + slab, 1), :] = top
    for o in (0, 1):
        code[pl.ds(BLOCK * o + 64 * SLABS, SLABS), :] = tops[pl.ds(SLABS * o, SLABS), :].astype(jnp.bfloat16)
    for one in copies[-2:]:
        one.wait()
    gain = (gains[pl.ds(0, 1), :] + gains[pl.ds(1, 1), :]).astype(jnp.bfloat16).astype(jnp.float32)
    gain = jnp.concatenate([gain] * 8, axis=1)
    me = (lax.axis_index("z") * 4 + lax.axis_index("y")) * 2 + lax.axis_index("core")
    place = me * 4 + lax.axis_index("x")
    row = lax.broadcasted_iota(jnp.int32, (SLABS, 128), 0)
    lane = lax.broadcasted_iota(jnp.int32, (SLABS, 128), 1)
    sums[pl.ds(2 * SLABS, SLABS), :] = jnp.where(row * 8 + lane // 16 == place, gain, 0.0)


def stepped(*arrays):
    weights = pltpu.VMEM((64, D_MODEL), jnp.float32)
    return pl.pallas_call(
        step_kernel,
        out_shape=(
            weights,
            weights,
            jax.ShapeDtypeStruct((2 * BLOCK, 128), jnp.bfloat16),
            jax.ShapeDtypeStruct((3 * SLABS, 128), jnp.float32),
        ),
        in_specs=[HBM] * 8,
        out_specs=(VMEM,) * 4,
        scratch_shapes=[pltpu.VMEM((64, D_MODEL), jnp.float32)] * 6
        + [pltpu.SemaphoreType.DMA((26,)), pltpu.VMEM((2 * SLABS, 128), jnp.float32), pltpu.VMEM((2, 16), jnp.float32)],
        compiler_params=pltpu.CompilerParams(vmem_limit_bytes=8 << 20),
        name="step",
    )(*(pltpu.with_memory_space_constraint(a, pltpu.HBM) for a in arrays))


def pack_kernel(spans, *refs):
    out, at = refs[-1], 0
    for ref, (lo, n) in zip(refs, spans):
        for k in range(0, n, 208):
            out[pl.ds(at + k, 208), :] = ref[pl.ds(lo + k, 208), :]
        at += n


def packed(*parts):
    spans = tuple((lo * BLOCK, n * BLOCK) for _, lo, n in parts)
    return pl.pallas_call(
        functools.partial(pack_kernel, spans),
        out_shape=jax.ShapeDtypeStruct((sum(n for _, n in spans), 128), jnp.bfloat16),
        in_specs=[VMEM] * len(parts),
        out_specs=VMEM,
        compiler_params=pltpu.CompilerParams(vmem_limit_bytes=2 << 20),
        name="pack",
    )(*(a for a, _, _ in parts))


def home(core_away, a, b):
    z, y, c = (lax.axis_index(axis) for axis in ROWS)
    c = lax.rem(c + core_away, 2)
    dz, dy = a + (b - a) * (1 - c), b + (a - b) * (1 - c)
    at = (lax.rem(z + 4 - dz, 4) * 4 + lax.rem(y + 4 - dy, 4)) * 2 + c
    return pl.ds(pl.multiple_of(at * 64, 64), 64)


def decode_kernel(plan, n, n_kept, n_out, *refs):
    arrays, total, extra = refs[:n], refs[n], refs[n + 1 : n + 1 + n_kept]
    plain, factor, sem = refs[-3:]
    got = refs[len(refs) - 3 - n_out : -3]
    outs, kept = got[:2], got[2:]
    blocks = [(ref, k, away, block) for ref, (name, away) in zip(arrays, plan) for k, block in enumerate(HELD[name])]
    copies = [pltpu.make_async_copy(a, b, sem.at[len(blocks) + i]) for i, (a, b) in enumerate(zip(extra, kept))]
    for one in copies:
        one.start()
    for n, (ref, k, away, (o, a, b)) in enumerate(blocks):
        factor[...] = ref[pl.ds(k * BLOCK + 64 * SLABS, SLABS), :].astype(jnp.float32) * (
            (D_MODEL / OCTAVES / math.log(2.0)) / total[pl.ds(SLABS * o, SLABS), :]
        )

        def slab(j, carry, ref=ref, at=k * BLOCK, to=64 * n):
            rows = pl.ds(pl.multiple_of(at + j * 64, 16), 64)
            value = jnp.log(ref[rows, :].astype(jnp.float32)) * factor[pl.ds(j, 1), :]
            plain[pl.ds(to, 64), pl.ds(pl.multiple_of(j * 128, 128), 128)] = value.astype(jnp.bfloat16)
            return carry

        lax.fori_loop(0, SLABS, slab, 0, unroll=UNROLL)
        one = pltpu.make_async_copy(plain.at[pl.ds(64 * n, 64), :], outs[o].at[home(away, a, b), :], sem.at[n])
        one.start()
        copies.append(one)
    for one in copies:
        one.wait()


def decoded(outs, arrays, plan, total, extra=()):
    n, aliased = len(arrays), 2 * (outs is not None)
    blocks = sum(len(HELD[name]) for name, _ in plan)
    out_shape = (READY, READY) + tuple(jax.ShapeDtypeStruct(a.shape, a.dtype) for a in extra)
    got = pl.pallas_call(
        functools.partial(decode_kernel, plan, n, len(extra), len(out_shape)),
        out_shape=out_shape,
        in_specs=[VMEM] * (n + 1 + len(extra)) + [HBM] * aliased,
        out_specs=(HBM,) * len(out_shape),
        scratch_shapes=[
            pltpu.VMEM((64 * blocks, D_MODEL), jnp.bfloat16),
            pltpu.VMEM((SLABS, 128), jnp.float32),
            pltpu.SemaphoreType.DMA((blocks + len(extra),)),
        ],
        input_output_aliases={n + 1 + len(extra) + i: i for i in range(aliased)},
        compiler_params=pltpu.CompilerParams(vmem_limit_bytes=(1 << 20) + 64 * blocks * D_MODEL * 2),
    )(*arrays, total, *extra, *(outs if aliased else ()))
    return got[:2], got[2:]


def local(w_gate, first_gate, second_gate, w_up, first_up, second_up, norm_train, norm_step):
    latest_gate, latest_up, own, sums = stepped(
        w_gate, first_gate, second_gate, w_up, first_up, second_up, norm_train[None], norm_step[None]
    )
    r, l = near(own, 1), near(own, 3)
    o = packed((near(packed((r, 0, 1)), 1), 0, 1), (near(packed((l, 1, 1)), 3), 0, 1))
    sums = sums + far(sums, 1) + far(sums, 3) + far(sums, 2)
    norm = sums[2 * SLABS :]
    for to in ((1, 0, 3, 2), (3, 2, 1, 0)):
        other = lax.ppermute(norm, "x", list(enumerate(to)))
        norm = norm + other
    sums = jnp.concatenate((sums[: 2 * SLABS], norm), axis=0)
    sums = sums + near(sums, 1) + near(sums, 3) + near(sums, 2)
    sums = sums + swapped(sums)
    total = sums[: 2 * SLABS]
    column_gate = total[:SLABS].reshape(D_MODEL) / D_MODEL
    column_up = total[SLABS:].reshape(D_MODEL) / D_MODEL
    serve_norm = sums[2 * SLABS :].reshape(D_MODEL).astype(jnp.bfloat16)

    first = packed(*((a, at, 1) for at in (0, 1) for a in (r, l)))
    got = {}
    for by in (1, 3):
        for name, value in (("fa", own), ("f1", first), ("f2", o)):
            got[name, by] = far(value, by)
    halves = ((0, 1), (1, 3))
    g1 = [far(packed((got["fa", by], half, 1), (got["f1", by], 2 * half, 2)), by) for half, by in halves]
    g2 = [far(packed((got["f2", by], half, 1)), by) for half, by in halves]
    mine = {
        "a": packed(*((a, at, 1) for at in (0, 1) for a in (own, r, l))),
        "b": packed(*((got["fa", by], 0, 2) for by in (1, 3)), *((got["f1", by], 0, 4) for by in (1, 3))),
        "c": packed((o, 0, 2), *((got["f2", by], 0, 2) for by in (1, 3))),
        "g1": packed(*((a, 0, 3) for a in g1)),
        "g2": packed(*((a, 0, 1) for a in g2)),
    }
    held = (mine, {name: swapped(value) for name, value in mine.items()})
    outs = None
    for label, plan in DECODES.items():
        extra = {"dec_0": (latest_gate, latest_up), "dec_1": (column_gate, column_up), "dec_3": (serve_norm,)}.get(label, ())
        outs, kept = decoded(outs, [held[away][name] for name, away in plan], plan, total, extra)
        if label == "dec_0":
            latest_gate, latest_up = kept
        if label == "dec_1":
            column_gate, column_up = kept
        if label == "dec_3":
            (serve_norm,) = kept
    return (outs[0], outs[1], column_gate, column_up, serve_norm, latest_gate, latest_up)


def solution(mesh):
    torus = Mesh(mesh.devices.reshape(4, 4, 2, mesh.shape["cols"]), ALL)
    whole = P(ROWS, "x")
    return jax.shard_map(
        local,
        mesh=torus,
        in_specs=(whole,) * 6 + (P(ALL),) * 2,
        out_specs=(P(None, "x"), P(None, "x"), P("x"), P("x"), P(), whole, whole),
        check_vma=False,
    )
```

profile of v0, /device:TPU:1, one launch (start us, length us, event | category | flops | bytes accessed | tf_op | source)
XLA Modules:
  0.0 119.4 jit_solution(8953048337596225983)
XLA Ops:
  0.6 2.4 %step.1 = (f32[64,2048]{1,0:T(8,128)S(1)}, f32[64,2048]{1,0:T(8,128)S(1)}, bf16[2080,128]{1,0:T(8,128)(2,1)S(1)}, f32[48,128]{1,0:T(8,128)S(1)}) custom-call(f32[64,2048]{1,0:T(8,128)} %w_g.1, f32[64,2048]{1,0:T(8,128)} %f_g.1, f32[64,2048]{1,0:T(8,128)} %s_g.1, f32[64,2048]{1,0:T(8,128)} %w_u.1, f32[64,2048]{1,0:T(8,128)} %f_u.1, f32[64,2048]{1,0:T(8,128)} %s_u.1, ...), custom_call_target="tpu_custom_call" | custom-call | tf_op jit(solution)/shard_map/step/pallas_call | solution.py:114
  3.1 2.5 %collective-permute-start = (bf16[2080,128]{1,0:T(8,128)(2,1)S(1)}, bf16[2080,128]{1,0:T(8,128)(2,1)S(1)}, u32[]{:S(2)}, u32[]{:S(2)}) collective-permute-start(bf16[2080,128]{1,0:T(8,128)(2,1)S(1)} %get-tuple-element.28.refs_0_.refs_3_), channel_id=1, source_target_pairs={{0,8},{4,36},{8,16},{12,44},{16,24},{20,52},{24,0},{28,60},{32,40}... | collective-permute-start | bytes 1597448 | tf_op jit(solution)/shard_map/ppermute | solution.py:58
  5.6 2.2 %collective-permute-start.2 = (bf16[2080,128]{1,0:T(8,128)(2,1)S(1)}, bf16[2080,128]{1,0:T(8,128)(2,1)S(1)}, u32[]{:S(2)}, u32[]{:S(2)}) collective-permute-start(bf16[2080,128]{1,0:T(8,128)(2,1)S(1)} %get-tuple-element.28.refs_0_.refs_3_), channel_id=1, source_target_pairs={{0,24},{4,100},{8,0},{12,108},{16,8},{20,116},{24,16},{28,124},{32... | collective-permute-start | bytes 1597448 | tf_op jit(solution)/shard_map/ppermute | solution.py:58
  7.8 6.8 %collective-permute-done.refs_0_.refs_2_.refs_1_.refs_4_ = bf16[2080,128]{1,0:T(8,128)(2,1)S(1)} collective-permute-done((bf16[2080,128]{1,0:T(8,128)(2,1)S(1)}, bf16[2080,128]{1,0:T(8,128)(2,1)S(1)}, u32[]{:S(2)}, u32[]{:S(2)}) %collective-permute-start) | collective-permute-done | bytes 532512 | tf_op jit(solution)/shard_map/ppermute | solution.py:58
  15.8 1.8 %collective-permute-start.22 = (bf16[4160,128]{1,0:T(8,128)(2,1)S(1)}, bf16[4160,128]{1,0:T(8,128)(2,1)S(1)}, u32[]{:S(2)}, u32[]{:S(2)}) collective-permute-start(bf16[4160,128]{1,0:T(8,128)(2,1)S(1)} %pack.19), channel_id=1, source_target_pairs={{0,96},{4,28},{8,104},{12,4},{16,112},{20,12},{24,120},{28,20},{32... | collective-permute-start | bytes 3194888 | tf_op jit(solution)/shard_map/ppermute | solution.py:62
  17.6 2.7 %collective-permute-start.21 = (bf16[2080,128]{1,0:T(8,128)(2,1)S(1)}, bf16[2080,128]{1,0:T(8,128)(2,1)S(1)}, u32[]{:S(2)}, u32[]{:S(2)}) collective-permute-start(bf16[2080,128]{1,0:T(8,128)(2,1)S(1)} %get-tuple-element.28.refs_0_.refs_3_), channel_id=1, source_target_pairs={{0,96},{4,28},{8,104},{12,4},{16,112},{20,12},{24,120},{28,20},{32... | collective-permute-start | bytes 1597448 | tf_op jit(solution)/shard_map/ppermute | solution.py:62
  20.3 15.6 %collective-permute-done.18.refs_0_ = bf16[2080,128]{1,0:T(8,128)(2,1)S(1)} collective-permute-done((bf16[2080,128]{1,0:T(8,128)(2,1)S(1)}, bf16[2080,128]{1,0:T(8,128)(2,1)S(1)}, u32[]{:S(2)}, u32[]{:S(2)}) %collective-permute-start.18) | collective-permute-done | bytes 532512 | tf_op jit(solution)/shard_map/ppermute | solution.py:62
  36.1 2.5 %collective-permute-start.26 = (bf16[12480,128]{1,0:T(8,128)(2,1)S(1)}, bf16[12480,128]{1,0:T(8,128)(2,1)S(1)}, u32[]{:S(2)}, u32[]{:S(2)}) collective-permute-start(bf16[12480,128]{1,0:T(8,128)(2,1)S(1)} %pack.24.refs_0_), channel_id=1, source_target_pairs={{0,4},{4,0},{1,5},{5,1},{2,6},{6,2},{3,7},{7,3},{8,12},{12,8},{9,1... | collective-permute-start | bytes 9584648 | tf_op jit(solution)/shard_map/ppermute | solution.py:66
  38.6 1.6 %collective-permute-start.1 = (bf16[1040,128]{1,0:T(8,128)(2,1)S(1)}, bf16[1040,128]{1,0:T(8,128)(2,1)S(1)}, u32[]{:S(2)}, u32[]{:S(2)}) collective-permute-start(bf16[1040,128]{1,0:T(8,128)(2,1)S(1)} %pack.13), channel_id=1, source_target_pairs={{0,8},{4,36},{8,16},{12,44},{16,24},{20,52},{24,0},{28,60},{32,40}... | collective-permute-start | bytes 798728 | tf_op jit(solution)/shard_map/ppermute | solution.py:58
  40.3 1.6 %collective-permute-start.3 = (bf16[1040,128]{1,0:T(8,128)(2,1)S(1)}, bf16[1040,128]{1,0:T(8,128)(2,1)S(1)}, u32[]{:S(2)}, u32[]{:S(2)}) collective-permute-start(bf16[1040,128]{1,0:T(8,128)(2,1)S(1)} %pack.14), channel_id=1, source_target_pairs={{0,24},{4,100},{8,0},{12,108},{16,8},{20,116},{24,16},{28,124},{32... | collective-permute-start | bytes 798728 | tf_op jit(solution)/shard_map/ppermute | solution.py:58
  45.9 1.7 %collective-permute-start.4 = (bf16[2080,128]{1,0:T(8,128)(2,1)S(1)}, bf16[2080,128]{1,0:T(8,128)(2,1)S(1)}, u32[]{:S(2)}, u32[]{:S(2)}) collective-permute-start(bf16[2080,128]{1,0:T(8,128)(2,1)S(1)} %pack.15.refs_0_), channel_id=1, source_target_pairs={{0,32},{4,12},{8,40},{12,20},{16,48},{20,28},{24,56},{28,4},{32,64... | collective-permute-start | bytes 1597448 | tf_op jit(solution)/shard_map/ppermute | solution.py:62
  49.0 11.2 %collective-permute-done.4.refs_0_.refs_1_ = bf16[2080,128]{1,0:T(8,128)(2,1)S(1)} collective-permute-done((bf16[2080,128]{1,0:T(8,128)(2,1)S(1)}, bf16[2080,128]{1,0:T(8,128)(2,1)S(1)}, u32[]{:S(2)}, u32[]{:S(2)}) %collective-permute-start.4) | collective-permute-done | bytes 532512 | tf_op jit(solution)/shard_map/ppermute | solution.py:62
  63.8 2.0 %collective-permute-start.27 = (bf16[6240,128]{1,0:T(8,128)(2,1)S(1)}, bf16[6240,128]{1,0:T(8,128)(2,1)S(1)}, u32[]{:S(2)}, u32[]{:S(2)}) collective-permute-start(bf16[6240,128]{1,0:T(8,128)(2,1)S(1)} %pack.25.refs_0_), channel_id=1, source_target_pairs={{0,4},{4,0},{1,5},{5,1},{2,6},{6,2},{3,7},{7,3},{8,12},{12,8},{9,1... | collective-permute-start | bytes 4792328 | tf_op jit(solution)/shard_map/ppermute | solution.py:66
  66.1 2.6 %collective-permute-start.24 = (bf16[6240,128]{1,0:T(8,128)(2,1)S(1)}, bf16[6240,128]{1,0:T(8,128)(2,1)S(1)}, u32[]{:S(2)}, u32[]{:S(2)}) collective-permute-start(bf16[6240,128]{1,0:T(8,128)(2,1)S(1)} %pack.22.refs_0_), channel_id=1, source_target_pairs={{0,4},{4,0},{1,5},{5,1},{2,6},{6,2},{3,7},{7,3},{8,12},{12,8},{9,1... | collective-permute-start | bytes 4792328 | tf_op jit(solution)/shard_map/ppermute | solution.py:66
  71.3 2.5 %collective-permute-start.13 = (f32[16,128]{1,0:T(8,128)S(1)}, f32[16,128]{1,0:T(8,128)S(1)}, u32[]{:S(2)}, u32[]{:S(2)}) collective-permute-start(f32[16,128]{1,0:T(8,128)S(1)} %slice_add_fusion), channel_id=1, source_target_pairs={{0,3},{1,2},{2,1},{3,0},{4,7},{5,6},{6,5},{7,4},{8,11},{9,10},{10,... | collective-permute-start | bytes 24584 | tf_op jit(solution)/shard_map/ppermute | solution.py:216
  75.0 3.9 %collective-permute-done.14 = f32[48,128]{1,0:T(8,128)S(1)} collective-permute-done((f32[48,128]{1,0:T(8,128)S(1)}, f32[48,128]{1,0:T(8,128)S(1)}, u32[]{:S(2)}, u32[]{:S(2)}) %collective-permute-start.14) | collective-permute-done | bytes 24608 | tf_op jit(solution)/shard_map/ppermute | solution.py:58
  78.9 2.7 %collective-permute-done.15 = f32[48,128]{1,0:T(8,128)S(1)} collective-permute-done((f32[48,128]{1,0:T(8,128)S(1)}, f32[48,128]{1,0:T(8,128)S(1)}, u32[]{:S(2)}, u32[]{:S(2)}) %collective-permute-start.15) | collective-permute-done | bytes 24608 | tf_op jit(solution)/shard_map/ppermute | solution.py:58
  81.7 4.1 %collective-permute-done.16 = f32[48,128]{1,0:T(8,128)S(1)} collective-permute-done((f32[48,128]{1,0:T(8,128)S(1)}, f32[48,128]{1,0:T(8,128)S(1)}, u32[]{:S(2)}, u32[]{:S(2)}) %collective-permute-start.16) | collective-permute-done | bytes 24608 | tf_op jit(solution)/shard_map/ppermute | solution.py:58
  86.3 6.4 %collective-permute-done.5.refs_0_ = bf16[1040,128]{1,0:T(8,128)(2,1)S(1)} collective-permute-done((bf16[1040,128]{1,0:T(8,128)(2,1)S(1)}, bf16[1040,128]{1,0:T(8,128)(2,1)S(1)}, u32[]{:S(2)}, u32[]{:S(2)}) %collective-permute-start.5) | collective-permute-done | bytes 266272 | tf_op jit(solution)/shard_map/ppermute | solution.py:62
  93.4 4.8 %collective-permute-done.7.refs_1_ = bf16[1040,128]{1,0:T(8,128)(2,1)S(1)} collective-permute-done((bf16[1040,128]{1,0:T(8,128)(2,1)S(1)}, bf16[1040,128]{1,0:T(8,128)(2,1)S(1)}, u32[]{:S(2)}, u32[]{:S(2)}) %collective-permute-start.7) | collective-permute-done | bytes 266272 | tf_op jit(solution)/shard_map/ppermute | solution.py:62
  98.2 8.9 %collective-permute-start.17 = (f32[48,128]{1,0:T(8,128)S(1)}, f32[48,128]{1,0:T(8,128)S(1)}, u32[]{:S(2)}, u32[]{:S(2)}) collective-permute-start(f32[48,128]{1,0:T(8,128)S(1)} %add_add_fusion), channel_id=1, source_target_pairs={{0,4},{4,0},{1,5},{5,1},{2,6},{6,2},{3,7},{7,3},{8,12},{12,8},{9,1... | collective-permute-start | bytes 73736 | tf_op jit(solution)/shard_map/ppermute | solution.py:66
  108.3 2.1 %shard_map.135 = (bf16[2048,2048]{1,0:T(8,128)(2,1)}, bf16[2048,2048]{1,0:T(8,128)(2,1)}, f32[64,2048]{1,0:T(8,128)}, f32[64,2048]{1,0:T(8,128)}) custom-call(bf16[6240,128]{1,0:T(8,128)(2,1)S(1)} %pack.25.refs_0_, bf16[6240,128]{1,0:T(8,128)(2,1)S(1)} %collective-permute-done.27.refs_1_, f32[32,128]{1,0:T(8,128)S(1)} %slice.29.refs_2_.refs_1_, ...), custom_call_target="tpu_custom_call" | custom-call | tf_op jit(solution)/shard_map/pallas_call | solution.py:191
  110.4 3.1 %shard_map.136 = (bf16[2048,2048]{1,0:T(8,128)(2,1)}, bf16[2048,2048]{1,0:T(8,128)(2,1)}, f32[2048]{0:T(1024)}, f32[2048]{0:T(1024)}) custom-call(bf16[12480,128]{1,0:T(8,128)(2,1)S(1)} %pack.24.refs_0_, bf16[12480,128]{1,0:T(8,128)(2,1)S(1)} %collective-permute-done.26.refs_1_, ...), custom_call_target="tpu_custom_call", output_to_operand_aliasing={{0}: (5, {}), {1}: (6, {})} | custom-call | tf_op jit(solution)/shard_map/pallas_call | solution.py:191
  113.6 1.9 %shard_map.137 = (bf16[2048,2048]{1,0:T(8,128)(2,1)}, bf16[2048,2048]{1,0:T(8,128)(2,1)}) custom-call(bf16[6240,128]{1,0:T(8,128)(2,1)S(1)} %pack.23.refs_0_, bf16[6240,128]{1,0:T(8,128)(2,1)S(1)} %collective-permute-done.25.refs_1_, f32[32,128]{1,0:T(8,128)S(1)} %slice.29.refs_2_.refs_1_, ...), custom_call_target="tpu_custom_call", output_to_operand_aliasing={{0}: (3, {}), {1}: (4, {})} | custom-call | tf_op jit(solution)/shard_map/pallas_call | solution.py:191
  (63 shorter events, 20.8 us)
Async XLA Ops:
  3.1 11.5 %collective-permute-start = (bf16[2080,128]{1,0:T(8,128)(2,1)S(1)}, bf16[2080,128]{1,0:T(8,128)(2,1)S(1)}, u32[]{:S(2)}, u32[]{:S(2)}) collective-permute-start(bf16[2080,128]{1,0:T(8,128)(2,1)S(1)} %get-tuple-element.28.refs_0_.refs_3_), channel_id=1, source_target_pairs={{0,8},{4,36},{8,16},{12,44},{16,24},{20,52},{24,0},{28,60},{32,40}... | collective-permute-start | bytes 1597448 | tf_op jit(solution)/shard_map/ppermute | solution.py:58
  5.6 9.0 %collective-permute-start.2 = (bf16[2080,128]{1,0:T(8,128)(2,1)S(1)}, bf16[2080,128]{1,0:T(8,128)(2,1)S(1)}, u32[]{:S(2)}, u32[]{:S(2)}) collective-permute-start(bf16[2080,128]{1,0:T(8,128)(2,1)S(1)} %get-tuple-element.28.refs_0_.refs_3_), channel_id=1, source_target_pairs={{0,24},{4,100},{8,0},{12,108},{16,8},{20,116},{24,16},{28,124},{32... | collective-permute-start | bytes 1597448 | tf_op jit(solution)/shard_map/ppermute | solution.py:58
  14.7 21.2 %collective-permute-start.19 = (bf16[4160,128]{1,0:T(8,128)(2,1)S(1)}, bf16[4160,128]{1,0:T(8,128)(2,1)S(1)}, u32[]{:S(2)}, u32[]{:S(2)}) collective-permute-start(bf16[4160,128]{1,0:T(8,128)(2,1)S(1)} %pack.19), channel_id=1, source_target_pairs={{0,32},{4,12},{8,40},{12,20},{16,48},{20,28},{24,56},{28,4},{32,64... | collective-permute-start | bytes 3194888 | tf_op jit(solution)/shard_map/ppermute | solution.py:62
  15.8 20.1 %collective-permute-start.22 = (bf16[4160,128]{1,0:T(8,128)(2,1)S(1)}, bf16[4160,128]{1,0:T(8,128)(2,1)S(1)}, u32[]{:S(2)}, u32[]{:S(2)}) collective-permute-start(bf16[4160,128]{1,0:T(8,128)(2,1)S(1)} %pack.19), channel_id=1, source_target_pairs={{0,96},{4,28},{8,104},{12,4},{16,112},{20,12},{24,120},{28,20},{32... | collective-permute-start | bytes 3194888 | tf_op jit(solution)/shard_map/ppermute | solution.py:62
  17.6 18.3 %collective-permute-start.18 = (bf16[2080,128]{1,0:T(8,128)(2,1)S(1)}, bf16[2080,128]{1,0:T(8,128)(2,1)S(1)}, u32[]{:S(2)}, u32[]{:S(2)}) collective-permute-start(bf16[2080,128]{1,0:T(8,128)(2,1)S(1)} %get-tuple-element.28.refs_0_.refs_3_), channel_id=1, source_target_pairs={{0,32},{4,12},{8,40},{12,20},{16,48},{20,28},{24,56},{28,4},{32,64... | collective-permute-start | bytes 1597448 | tf_op jit(solution)/shard_map/ppermute | solution.py:62
  17.6 18.3 %collective-permute-start.21 = (bf16[2080,128]{1,0:T(8,128)(2,1)S(1)}, bf16[2080,128]{1,0:T(8,128)(2,1)S(1)}, u32[]{:S(2)}, u32[]{:S(2)}) collective-permute-start(bf16[2080,128]{1,0:T(8,128)(2,1)S(1)} %get-tuple-element.28.refs_0_.refs_3_), channel_id=1, source_target_pairs={{0,96},{4,28},{8,104},{12,4},{16,112},{20,12},{24,120},{28,20},{32... | collective-permute-start | bytes 1597448 | tf_op jit(solution)/shard_map/ppermute | solution.py:62
  36.1 74.3 %collective-permute-start.26 = (bf16[12480,128]{1,0:T(8,128)(2,1)S(1)}, bf16[12480,128]{1,0:T(8,128)(2,1)S(1)}, u32[]{:S(2)}, u32[]{:S(2)}) collective-permute-start(bf16[12480,128]{1,0:T(8,128)(2,1)S(1)} %pack.24.refs_0_), channel_id=1, source_target_pairs={{0,4},{4,0},{1,5},{5,1},{2,6},{6,2},{3,7},{7,3},{8,12},{12,8},{9,1... | collective-permute-start | bytes 9584648 | tf_op jit(solution)/shard_map/ppermute | solution.py:66
  38.6 7.2 %collective-permute-start.1 = (bf16[1040,128]{1,0:T(8,128)(2,1)S(1)}, bf16[1040,128]{1,0:T(8,128)(2,1)S(1)}, u32[]{:S(2)}, u32[]{:S(2)}) collective-permute-start(bf16[1040,128]{1,0:T(8,128)(2,1)S(1)} %pack.13), channel_id=1, source_target_pairs={{0,8},{4,36},{8,16},{12,44},{16,24},{20,52},{24,0},{28,60},{32,40}... | collective-permute-start | bytes 798728 | tf_op jit(solution)/shard_map/ppermute | solution.py:58
  40.3 5.6 %collective-permute-start.3 = (bf16[1040,128]{1,0:T(8,128)(2,1)S(1)}, bf16[1040,128]{1,0:T(8,128)(2,1)S(1)}, u32[]{:S(2)}, u32[]{:S(2)}) collective-permute-start(bf16[1040,128]{1,0:T(8,128)(2,1)S(1)} %pack.14), channel_id=1, source_target_pairs={{0,24},{4,100},{8,0},{12,108},{16,8},{20,116},{24,16},{28,124},{32... | collective-permute-start | bytes 798728 | tf_op jit(solution)/shard_map/ppermute | solution.py:58
  41.9 21.1 %collective-permute-start.20 = (bf16[3120,128]{1,0:T(8,128)(2,1)S(1)}, bf16[3120,128]{1,0:T(8,128)(2,1)S(1)}, u32[]{:S(2)}, u32[]{:S(2)}) collective-permute-start(bf16[3120,128]{1,0:T(8,128)(2,1)S(1)} %pack.20), channel_id=1, source_target_pairs={{0,32},{4,12},{8,40},{12,20},{16,48},{20,28},{24,56},{28,4},{32,64... | collective-permute-start | bytes 2396168 | tf_op jit(solution)/shard_map/ppermute | solution.py:62
  43.3 20.5 %collective-permute-start.23 = (bf16[3120,128]{1,0:T(8,128)(2,1)S(1)}, bf16[3120,128]{1,0:T(8,128)(2,1)S(1)}, u32[]{:S(2)}, u32[]{:S(2)}) collective-permute-start(bf16[3120,128]{1,0:T(8,128)(2,1)S(1)} %pack.21), channel_id=1, source_target_pairs={{0,96},{4,28},{8,104},{12,4},{16,112},{20,12},{24,120},{28,20},{32... | collective-permute-start | bytes 2396168 | tf_op jit(solution)/shard_map/ppermute | solution.py:62
  45.9 14.3 %collective-permute-start.4 = (bf16[2080,128]{1,0:T(8,128)(2,1)S(1)}, bf16[2080,128]{1,0:T(8,128)(2,1)S(1)}, u32[]{:S(2)}, u32[]{:S(2)}) collective-permute-start(bf16[2080,128]{1,0:T(8,128)(2,1)S(1)} %pack.15.refs_0_), channel_id=1, source_target_pairs={{0,32},{4,12},{8,40},{12,20},{16,48},{20,28},{24,56},{28,4},{32,64... | collective-permute-start | bytes 1597448 | tf_op jit(solution)/shard_map/ppermute | solution.py:62
  47.7 14.0 %collective-permute-start.6 = (bf16[2080,128]{1,0:T(8,128)(2,1)S(1)}, bf16[2080,128]{1,0:T(8,128)(2,1)S(1)}, u32[]{:S(2)}, u32[]{:S(2)}) collective-permute-start(bf16[2080,128]{1,0:T(8,128)(2,1)S(1)} %pack.15.refs_0_), channel_id=1, source_target_pairs={{0,96},{4,28},{8,104},{12,4},{16,112},{20,12},{24,120},{28,20},{32... | collective-permute-start | bytes 1597448 | tf_op jit(solution)/shard_map/ppermute | solution.py:62
  60.2 5.7 %collective-permute-start.10 = (f32[48,128]{1,0:T(8,128)S(1)}, f32[48,128]{1,0:T(8,128)S(1)}, u32[]{:S(2)}, u32[]{:S(2)}) collective-permute-start(f32[48,128]{1,0:T(8,128)S(1)} %get-tuple-element.29), channel_id=1, source_target_pairs={{0,96},{4,28},{8,104},{12,4},{16,112},{20,12},{24,120},{28,20},{32... | collective-permute-start | bytes 73736 | tf_op jit(solution)/shard_map/ppermute | solution.py:62
  61.6 4.4 %collective-permute-start.11 = (f32[48,128]{1,0:T(8,128)S(1)}, f32[48,128]{1,0:T(8,128)S(1)}, u32[]{:S(2)}, u32[]{:S(2)}) collective-permute-start(f32[48,128]{1,0:T(8,128)S(1)} %get-tuple-element.29), channel_id=1, source_target_pairs={{0,64},{4,20},{8,72},{12,28},{16,80},{20,4},{24,88},{28,12},{32,96... | collective-permute-start | bytes 73736 | tf_op jit(solution)/shard_map/ppermute | solution.py:62
  63.0 5.7 %collective-permute-start.9 = (f32[48,128]{1,0:T(8,128)S(1)}, f32[48,128]{1,0:T(8,128)S(1)}, u32[]{:S(2)}, u32[]{:S(2)}) collective-permute-start(f32[48,128]{1,0:T(8,128)S(1)} %get-tuple-element.29), channel_id=1, source_target_pairs={{0,32},{4,12},{8,40},{12,20},{16,48},{20,28},{24,56},{28,4},{32,64... | collective-permute-start | bytes 73736 | tf_op jit(solution)/shard_map/ppermute | solution.py:62
  63.8 44.5 %collective-permute-start.27 = (bf16[6240,128]{1,0:T(8,128)(2,1)S(1)}, bf16[6240,128]{1,0:T(8,128)(2,1)S(1)}, u32[]{:S(2)}, u32[]{:S(2)}) collective-permute-start(bf16[6240,128]{1,0:T(8,128)(2,1)S(1)} %pack.25.refs_0_), channel_id=1, source_target_pairs={{0,4},{4,0},{1,5},{5,1},{2,6},{6,2},{3,7},{7,3},{8,12},{12,8},{9,1... | collective-permute-start | bytes 4792328 | tf_op jit(solution)/shard_map/ppermute | solution.py:66
  66.0 47.6 %collective-permute-start.25 = (bf16[6240,128]{1,0:T(8,128)(2,1)S(1)}, bf16[6240,128]{1,0:T(8,128)(2,1)S(1)}, u32[]{:S(2)}, u32[]{:S(2)}) collective-permute-start(bf16[6240,128]{1,0:T(8,128)(2,1)S(1)} %pack.23.refs_0_), channel_id=1, source_target_pairs={{0,4},{4,0},{1,5},{5,1},{2,6},{6,2},{3,7},{7,3},{8,12},{12,8},{9,1... | collective-permute-start | bytes 4792328 | tf_op jit(solution)/shard_map/ppermute | solution.py:66
  66.1 50.7 %collective-permute-start.24 = (bf16[6240,128]{1,0:T(8,128)(2,1)S(1)}, bf16[6240,128]{1,0:T(8,128)(2,1)S(1)}, u32[]{:S(2)}, u32[]{:S(2)}) collective-permute-start(bf16[6240,128]{1,0:T(8,128)(2,1)S(1)} %pack.22.refs_0_), channel_id=1, source_target_pairs={{0,4},{4,0},{1,5},{5,1},{2,6},{6,2},{3,7},{7,3},{8,12},{12,8},{9,1... | collective-permute-start | bytes 4792328 | tf_op jit(solution)/shard_map/ppermute | solution.py:66
  81.5 4.2 %collective-permute-start.16 = (f32[48,128]{1,0:T(8,128)S(1)}, f32[48,128]{1,0:T(8,128)S(1)}, u32[]{:S(2)}, u32[]{:S(2)}) collective-permute-start(f32[48,128]{1,0:T(8,128)S(1)} %pad_maximum_fusion), channel_id=1, source_target_pairs={{0,16},{4,68},{8,24},{12,76},{16,0},{20,84},{24,8},{28,92},{32,48}... | collective-permute-start | bytes 73736 | tf_op jit(solution)/shard_map/ppermute | solution.py:58
  85.7 6.9 %collective-permute-start.5 = (bf16[1040,128]{1,0:T(8,128)(2,1)S(1)}, bf16[1040,128]{1,0:T(8,128)(2,1)S(1)}, u32[]{:S(2)}, u32[]{:S(2)}) collective-permute-start(bf16[1040,128]{1,0:T(8,128)(2,1)S(1)} %pack.16), channel_id=1, source_target_pairs={{0,32},{4,12},{8,40},{12,20},{16,48},{20,28},{24,56},{28,4},{32,64... | collective-permute-start | bytes 798728 | tf_op jit(solution)/shard_map/ppermute | solution.py:62
  92.6 5.6 %collective-permute-start.7 = (bf16[1040,128]{1,0:T(8,128)(2,1)S(1)}, bf16[1040,128]{1,0:T(8,128)(2,1)S(1)}, u32[]{:S(2)}, u32[]{:S(2)}) collective-permute-start(bf16[1040,128]{1,0:T(8,128)(2,1)S(1)} %pack.17), channel_id=1, source_target_pairs={{0,96},{4,28},{8,104},{12,4},{16,112},{20,12},{24,120},{28,20},{32... | collective-permute-start | bytes 798728 | tf_op jit(solution)/shard_map/ppermute | solution.py:62
  98.2 9.7 %collective-permute-start.17 = (f32[48,128]{1,0:T(8,128)S(1)}, f32[48,128]{1,0:T(8,128)S(1)}, u32[]{:S(2)}, u32[]{:S(2)}) collective-permute-start(f32[48,128]{1,0:T(8,128)S(1)} %add_add_fusion), channel_id=1, source_target_pairs={{0,4},{4,0},{1,5},{5,1},{2,6},{6,2},{3,7},{7,3},{8,12},{12,8},{9,1... | collective-permute-start | bytes 73736 | tf_op jit(solution)/shard_map/ppermute | solution.py:66
  107.9 10.4 %collective-permute-start.8 = (bf16[2080,128]{1,0:T(8,128)(2,1)S(1)}, bf16[2080,128]{1,0:T(8,128)(2,1)S(1)}, u32[]{:S(2)}, u32[]{:S(2)}) collective-permute-start(bf16[2080,128]{1,0:T(8,128)(2,1)S(1)} %pack.18.refs_1_), channel_id=1, source_target_pairs={{0,4},{4,0},{1,5},{5,1},{2,6},{6,2},{3,7},{7,3},{8,12},{12,8},{9,1... | collective-permute-start | bytes 1597448 | tf_op jit(solution)/shard_map/ppermute | solution.py:66
  (4 other events, 12.9 us)
where the time goes:
time: 119 us
  waiting for transfers between devices  59.9 us (50%)
  starting transfers between devices  44.3 us (37%)
  Pallas kernels  14.1 us (12%)
    ppermute x13, waiting for transfers between devices, far(): return lax.ppermute(value, ROWS, near_far(0, by))  38 us
    ppermute x7, waiting for transfers between devices, near(): return lax.ppermute(value, ROWS, near_far(by, 0))  18.6 us
    ppermute x6, starting transfers between devices, swapped(): return lax.ppermute(value, 'core', [(0, 1), (1, 0)])  16.4 us
    ppermute x13, starting transfers between devices, far(): return lax.ppermute(value, ROWS, near_far(0, by))  16.1 us
    pallas_call x6, Pallas kernels, decoded(): pl.pallas_call(functools.partial(decode_kernel, plan, n, len(extra), len(...  10.8 us
    ppermute x7, starting transfers between devices, near(): return lax.ppermute(value, ROWS, near_far(by, 0))  8.01 us
    ppermute x2, starting transfers between devices, local(): other = lax.ppermute(norm, 'x', list(enumerate(to)))  3.77 us
    ppermute x2, waiting for transfers between devices, local(): other = lax.ppermute(norm, 'x', list(enumerate(to)))  2.52 us
  transfers between devices with their start and end apart: 28, of which 13 were waited for; matrix products, arithmetic and copies ran while one was open for 0% of the time, Pallas kernels for 9%

commit v1 on v0

--- a/solution.py
+++ b/solution.py
@@ -28,15 +28,16 @@
     "dec_0": (("a", 0), ("a", 1)),
     "dec_1": (("b", 0), ("b", 1)),
     "dec_2": (("c", 0), ("c", 1)),
-    "dec_3": (("g1", 0),),
-    "dec_4": (("g1", 1), ("g2", 0)),
+    "dec_3": (("g1a", 0), ("g1b", 0)),
+    "dec_4": (("g1a", 1), ("g1b", 1), ("g2", 0)),
     "dec_5": (("g2", 1),),
 }
 HELD = {
     "a": [(o, a, 0) for o in (0, 1) for a in (0, 1, 3)],
     "b": [(o, 0, b) for b in (1, 3) for o in (0, 1)] + [(o, a, b) for b in (1, 3) for o in (0, 1) for a in (1, 3)],
     "c": [(o, 2, b) for b in (0, 1, 3) for o in (0, 1)],
-    "g1": [(o, a, 2) for o in (0, 1) for a in (0, 1, 3)],
+    "g1a": [(0, a, 2) for a in (0, 1, 3)],
+    "g1b": [(1, a, 2) for a in (0, 1, 3)],
     "g2": [(o, 2, 2) for o in (0, 1)],
 }
 
@@ -68,7 +69,7 @@
 
 def step_kernel(w_g, f_g, s_g, w_u, f_u, s_u, norm, change, latest_g, latest_u, code, sums, *scratch):
     held, sem, tops, gains = scratch[:6], scratch[6], scratch[7], scratch[8]
-    wide = 512
+    wide = 1024
     chunks = D_MODEL // wide
     sources = (w_g, f_g, s_g, w_u, f_u, s_u)
     copies = []
@@ -122,7 +123,7 @@
         in_specs=[HBM] * 8,
         out_specs=(VMEM,) * 4,
         scratch_shapes=[pltpu.VMEM((64, D_MODEL), jnp.float32)] * 6
-        + [pltpu.SemaphoreType.DMA((26,)), pltpu.VMEM((2 * SLABS, 128), jnp.float32), pltpu.VMEM((2, 16), jnp.float32)],
+        + [pltpu.SemaphoreType.DMA((14,)), pltpu.VMEM((2 * SLABS, 128), jnp.float32), pltpu.VMEM((2, 16), jnp.float32)],
         compiler_params=pltpu.CompilerParams(vmem_limit_bytes=8 << 20),
         name="step",
     )(*(pltpu.with_memory_space_constraint(a, pltpu.HBM) for a in arrays))
@@ -235,7 +236,8 @@
         "a": packed(*((a, at, 1) for at in (0, 1) for a in (own, r, l))),
         "b": packed(*((got["fa", by], 0, 2) for by in (1, 3)), *((got["f1", by], 0, 4) for by in (1, 3))),
         "c": packed((o, 0, 2), *((got["f2", by], 0, 2) for by in (1, 3))),
-        "g1": packed(*((a, 0, 3) for a in g1)),
+        "g1a": g1[0],
+        "g1b": g1[1],
         "g2": packed(*((a, 0, 1) for a in g2)),
     }
     held = (mine, {name: swapped(value) for name, value in mine.items()})

time: 119 us -> 98 us (0.82)
  waiting for transfers between devices: 59.9 us -> 37.3 us
  starting transfers between devices: 44.3 us -> 45.7 us
    ppermute x13, waiting for transfers between devices: 38 us -> 25.8 us  [far(): return lax.ppermute(value, ROWS, near_far(0, by))]
    ppermute x7, waiting for transfers between devices: 18.6 us -> 8.83 us  [near(): return lax.ppermute(value, ROWS, near_far(by, 0))]
    ppermute x7, starting transfers between devices: 8.01 us -> 10.9 us  [near(): return lax.ppermute(value, ROWS, near_far(by, 0))]
    ppermute x6 -> x7, starting transfers between devices: 16.4 us -> 13.5 us  [swapped(): return lax.ppermute(value, 'core', [(0, 1), (1, 0)])]
    ppermute x13, starting transfers between devices: 16.1 us -> 17.9 us  [far(): return lax.ppermute(value, ROWS, near_far(0, by))]
  transfers between devices with their start and end apart: 28 -> 29, of which waited for: 13 -> 9; matrix products, arithmetic and copies ran while one was open for 0% -> 0% of each run, Pallas kernels for 9% -> 11%
where the time goes in v1:
time: 98 us; the launch traced here: 97.9 us
  starting transfers between devices  45.7 us (47%)
  waiting for transfers between devices  37.3 us (38%)
  Pallas kernels  13.8 us (14%)
  between operations  1.03 us (1%)
    ppermute x13, waiting for transfers between devices, far(): return lax.ppermute(value, ROWS, near_far(0, by))  25.8 us
    ppermute x13, starting transfers between devices, far(): return lax.ppermute(value, ROWS, near_far(0, by))  17.9 us
    ppermute x7, starting transfers between devices, swapped(): return lax.ppermute(value, 'core', [(0, 1), (1, 0)])  13.5 us
    ppermute x7, starting transfers between devices, near(): return lax.ppermute(value, ROWS, near_far(by, 0))  10.9 us
    pallas_call x6, Pallas kernels, decoded(): pl.pallas_call(functools.partial(decode_kernel, plan, n, len(extra), len(...  10.8 us
    ppermute x7, waiting for transfers between devices, near(): return lax.ppermute(value, ROWS, near_far(by, 0))  8.83 us
    ppermute x2, starting transfers between devices, local(): other = lax.ppermute(norm, 'x', list(enumerate(to)))  3.37 us
    pallas_call x1, Pallas kernels, stepped(): pl.pallas_call(step_kernel, out_shape=(weights, weights, jax.ShapeDtypeSt...  2.24 us
  transfers between devices with their start and end apart: 29, of which 9 were waited for; matrix products, arithmetic and copies ran while one was open for 0% of the time, Pallas kernels for 11%

profile of v1, /device:TPU:1, one launch (start us, length us, event | category | flops | bytes accessed | tf_op | source)
XLA Modules:
  0.0 97.9 jit_solution(9530248442255566827)
XLA Ops:
  0.6 2.2 %step.1 = (f32[64,2048]{1,0:T(8,128)S(1)}, f32[64,2048]{1,0:T(8,128)S(1)}, bf16[2080,128]{1,0:T(8,128)(2,1)S(1)}, f32[48,128]{1,0:T(8,128)S(1)}) custom-call(f32[64,2048]{1,0:T(8,128)} %w_g.1, f32[64,2048]{1,0:T(8,128)} %f_g.1, f32[64,2048]{1,0:T(8,128)} %s_g.1, f32[64,2048]{1,0:T(8,128)} %w_u.1, f32[64,2048]{1,0:T(8,128)} %f_u.1, f32[64,2048]{1,0:T(8,128)} %s_u.1, ...), custom_call_target="tpu_custom_call" | custom-call | tf_op jit(solution)/shard_map/step/pallas_call | solution.py:115
  2.9 2.5 %collective-permute-start = (bf16[2080,128]{1,0:T(8,128)(2,1)S(1)}, bf16[2080,128]{1,0:T(8,128)(2,1)S(1)}, u32[]{:S(2)}, u32[]{:S(2)}) collective-permute-start(bf16[2080,128]{1,0:T(8,128)(2,1)S(1)} %get-tuple-element.28.refs_0_.refs_3_), channel_id=1, source_target_pairs={{0,8},{4,36},{8,16},{12,44},{16,24},{20,52},{24,0},{28,60},{32,40}... | collective-permute-start | bytes 1597448 | tf_op jit(solution)/shard_map/ppermute | solution.py:59
  5.4 2.2 %collective-permute-start.2 = (bf16[2080,128]{1,0:T(8,128)(2,1)S(1)}, bf16[2080,128]{1,0:T(8,128)(2,1)S(1)}, u32[]{:S(2)}, u32[]{:S(2)}) collective-permute-start(bf16[2080,128]{1,0:T(8,128)(2,1)S(1)} %get-tuple-element.28.refs_0_.refs_3_), channel_id=1, source_target_pairs={{0,24},{4,100},{8,0},{12,108},{16,8},{20,116},{24,16},{28,124},{32... | collective-permute-start | bytes 1597448 | tf_op jit(solution)/shard_map/ppermute | solution.py:59
  7.6 6.8 %collective-permute-done.refs_0_.refs_2_.refs_1_.refs_4_ = bf16[2080,128]{1,0:T(8,128)(2,1)S(1)} collective-permute-done((bf16[2080,128]{1,0:T(8,128)(2,1)S(1)}, bf16[2080,128]{1,0:T(8,128)(2,1)S(1)}, u32[]{:S(2)}, u32[]{:S(2)}) %collective-permute-start) | collective-permute-done | bytes 532512 | tf_op jit(solution)/shard_map/ppermute | solution.py:59
  15.6 1.8 %collective-permute-start.23 = (bf16[4160,128]{1,0:T(8,128)(2,1)S(1)}, bf16[4160,128]{1,0:T(8,128)(2,1)S(1)}, u32[]{:S(2)}, u32[]{:S(2)}) collective-permute-start(bf16[4160,128]{1,0:T(8,128)(2,1)S(1)} %pack.18), channel_id=1, source_target_pairs={{0,96},{4,28},{8,104},{12,4},{16,112},{20,12},{24,120},{28,20},{32... | collective-permute-start | bytes 3194888 | tf_op jit(solution)/shard_map/ppermute | solution.py:63
  17.5 2.7 %collective-permute-start.22 = (bf16[2080,128]{1,0:T(8,128)(2,1)S(1)}, bf16[2080,128]{1,0:T(8,128)(2,1)S(1)}, u32[]{:S(2)}, u32[]{:S(2)}) collective-permute-start(bf16[2080,128]{1,0:T(8,128)(2,1)S(1)} %get-tuple-element.28.refs_0_.refs_3_), channel_id=1, source_target_pairs={{0,96},{4,28},{8,104},{12,4},{16,112},{20,12},{24,120},{28,20},{32... | collective-permute-start | bytes 1597448 | tf_op jit(solution)/shard_map/ppermute | solution.py:63
  20.1 15.6 %collective-permute-done.18.refs_0_ = bf16[2080,128]{1,0:T(8,128)(2,1)S(1)} collective-permute-done((bf16[2080,128]{1,0:T(8,128)(2,1)S(1)}, bf16[2080,128]{1,0:T(8,128)(2,1)S(1)}, u32[]{:S(2)}, u32[]{:S(2)}) %collective-permute-start.18) | collective-permute-done | bytes 532512 | tf_op jit(solution)/shard_map/ppermute | solution.py:63
  36.0 2.5 %collective-permute-start.27 = (bf16[12480,128]{1,0:T(8,128)(2,1)S(1)}, bf16[12480,128]{1,0:T(8,128)(2,1)S(1)}, u32[]{:S(2)}, u32[]{:S(2)}) collective-permute-start(bf16[12480,128]{1,0:T(8,128)(2,1)S(1)} %pack.22.refs_0_), channel_id=1, source_target_pairs={{0,4},{4,0},{1,5},{5,1},{2,6},{6,2},{3,7},{7,3},{8,12},{12,8},{9,1... | collective-permute-start | bytes 9584648 | tf_op jit(solution)/shard_map/ppermute | solution.py:67
  38.5 1.6 %collective-permute-start.1 = (bf16[1040,128]{1,0:T(8,128)(2,1)S(1)}, bf16[1040,128]{1,0:T(8,128)(2,1)S(1)}, u32[]{:S(2)}, u32[]{:S(2)}) collective-permute-start(bf16[1040,128]{1,0:T(8,128)(2,1)S(1)} %pack.12), channel_id=1, source_target_pairs={{0,8},{4,36},{8,16},{12,44},{16,24},{20,52},{24,0},{28,60},{32,40}... | collective-permute-start | bytes 798728 | tf_op jit(solution)/shard_map/ppermute | solution.py:59
  40.1 1.6 %collective-permute-start.3 = (bf16[1040,128]{1,0:T(8,128)(2,1)S(1)}, bf16[1040,128]{1,0:T(8,128)(2,1)S(1)}, u32[]{:S(2)}, u32[]{:S(2)}) collective-permute-start(bf16[1040,128]{1,0:T(8,128)(2,1)S(1)} %pack.13), channel_id=1, source_target_pairs={{0,24},{4,100},{8,0},{12,108},{16,8},{20,116},{24,16},{28,124},{32... | collective-permute-start | bytes 798728 | tf_op jit(solution)/shard_map/ppermute | solution.py:59
  41.7 2.6 %collective-permute-start.10 = (f32[48,128]{1,0:T(8,128)S(1)}, f32[48,128]{1,0:T(8,128)S(1)}, u32[]{:S(2)}, u32[]{:S(2)}) collective-permute-start(f32[48,128]{1,0:T(8,128)S(1)} %get-tuple-element.29), channel_id=1, source_target_pairs={{0,96},{4,28},{8,104},{12,4},{16,112},{20,12},{24,120},{28,20},{32... | collective-permute-start | bytes 73736 | tf_op jit(solution)/shard_map/ppermute | solution.py:63
  47.8 1.7 %collective-permute-start.6 = (bf16[2080,128]{1,0:T(8,128)(2,1)S(1)}, bf16[2080,128]{1,0:T(8,128)(2,1)S(1)}, u32[]{:S(2)}, u32[]{:S(2)}) collective-permute-start(bf16[2080,128]{1,0:T(8,128)(2,1)S(1)} %pack.14.refs_0_), channel_id=1, source_target_pairs={{0,96},{4,28},{8,104},{12,4},{16,112},{20,12},{24,120},{28,20},{32... | collective-permute-start | bytes 1597448 | tf_op jit(solution)/shard_map/ppermute | solution.py:63
  51.3 1.9 %collective-permute-start.28 = (bf16[6240,128]{1,0:T(8,128)(2,1)S(1)}, bf16[6240,128]{1,0:T(8,128)(2,1)S(1)}, u32[]{:S(2)}, u32[]{:S(2)}) collective-permute-start(bf16[6240,128]{1,0:T(8,128)(2,1)S(1)} %pack.23.refs_0_), channel_id=1, source_target_pairs={{0,4},{4,0},{1,5},{5,1},{2,6},{6,2},{3,7},{7,3},{8,12},{12,8},{9,1... | collective-permute-start | bytes 4792328 | tf_op jit(solution)/shard_map/ppermute | solution.py:67
  53.1 2.1 %collective-permute-start.13 = (f32[16,128]{1,0:T(8,128)S(1)}, f32[16,128]{1,0:T(8,128)S(1)}, u32[]{:S(2)}, u32[]{:S(2)}) collective-permute-start(f32[16,128]{1,0:T(8,128)S(1)} %slice_add_fusion), channel_id=1, source_target_pairs={{0,3},{1,2},{2,1},{3,0},{4,7},{5,6},{6,5},{7,4},{8,11},{9,10},{10,... | collective-permute-start | bytes 24584 | tf_op jit(solution)/shard_map/ppermute | solution.py:217
  55.2 1.9 %collective-permute-done.13 = f32[16,128]{1,0:T(8,128)S(1)} collective-permute-done((f32[16,128]{1,0:T(8,128)S(1)}, f32[16,128]{1,0:T(8,128)S(1)}, u32[]{:S(2)}, u32[]{:S(2)}) %collective-permute-start.13) | collective-permute-done | bytes 8224 | tf_op jit(solution)/shard_map/ppermute | solution.py:217
  57.2 2.7 %collective-permute-start.15 = (f32[48,128]{1,0:T(8,128)S(1)}, f32[48,128]{1,0:T(8,128)S(1)}, u32[]{:S(2)}, u32[]{:S(2)}) collective-permute-start(f32[48,128]{1,0:T(8,128)S(1)} %pad_maximum_fusion), channel_id=1, source_target_pairs={{0,24},{4,100},{8,0},{12,108},{16,8},{20,116},{24,16},{28,124},{32... | collective-permute-start | bytes 73736 | tf_op jit(solution)/shard_map/ppermute | solution.py:59
  61.1 2.6 %collective-permute-start.7 = (bf16[1040,128]{1,0:T(8,128)(2,1)S(1)}, bf16[1040,128]{1,0:T(8,128)(2,1)S(1)}, u32[]{:S(2)}, u32[]{:S(2)}) collective-permute-start(bf16[1040,128]{1,0:T(8,128)(2,1)S(1)} %pack.16), channel_id=1, source_target_pairs={{0,96},{4,28},{8,104},{12,4},{16,112},{20,12},{24,120},{28,20},{32... | collective-permute-start | bytes 798728 | tf_op jit(solution)/shard_map/ppermute | solution.py:63
  64.0 4.9 %collective-permute-start.17 = (f32[48,128]{1,0:T(8,128)S(1)}, f32[48,128]{1,0:T(8,128)S(1)}, u32[]{:S(2)}, u32[]{:S(2)}) collective-permute-start(f32[48,128]{1,0:T(8,128)S(1)} %add_add_fusion), channel_id=1, source_target_pairs={{0,4},{4,0},{1,5},{5,1},{2,6},{6,2},{3,7},{7,3},{8,12},{12,8},{9,1... | collective-permute-start | bytes 73736 | tf_op jit(solution)/shard_map/ppermute | solution.py:67
  70.3 2.7 %collective-permute-start.24 = (bf16[3120,128]{1,0:T(8,128)(2,1)S(1)}, bf16[3120,128]{1,0:T(8,128)(2,1)S(1)}, u32[]{:S(2)}, u32[]{:S(2)}) collective-permute-start(bf16[3120,128]{1,0:T(8,128)(2,1)S(1)} %pack.20), channel_id=1, source_target_pairs={{0,96},{4,28},{8,104},{12,4},{16,112},{20,12},{24,120},{28,20},{32... | collective-permute-start | bytes 2396168 | tf_op jit(solution)/shard_map/ppermute | solution.py:63
  73.0 9.8 %collective-permute-done.20.refs_0_ = bf16[3120,128]{1,0:T(8,128)(2,1)S(1)} collective-permute-done((bf16[3120,128]{1,0:T(8,128)(2,1)S(1)}, bf16[3120,128]{1,0:T(8,128)(2,1)S(1)}, u32[]{:S(2)}, u32[]{:S(2)}) %collective-permute-start.20) | collective-permute-done | bytes 798752 | tf_op jit(solution)/shard_map/ppermute | solution.py:63
  82.8 3.2 %collective-permute-start.21 = (bf16[3120,128]{1,0:T(8,128)(2,1)S(1)}, bf16[3120,128]{1,0:T(8,128)(2,1)S(1)}, u32[]{:S(2)}, u32[]{:S(2)}) collective-permute-start(bf16[3120,128]{1,0:T(8,128)(2,1)S(1)} %collective-permute-done.20.refs_0_), channel_id=1, source_target_pairs={{0,4},{4,0},{1,5},{5,1},{2,6},{6,2},{3,7},{7,3},{8,12},{12,8},{9,1... | collective-permute-start | bytes 2396168 | tf_op jit(solution)/shard_map/ppermute | solution.py:67
  86.8 2.1 %shard_map.135 = (bf16[2048,2048]{1,0:T(8,128)(2,1)}, bf16[2048,2048]{1,0:T(8,128)(2,1)}, f32[64,2048]{1,0:T(8,128)}, f32[64,2048]{1,0:T(8,128)}) custom-call(bf16[6240,128]{1,0:T(8,128)(2,1)S(1)} %pack.23.refs_0_, bf16[6240,128]{1,0:T(8,128)(2,1)S(1)} %collective-permute-done.28.refs_1_, f32[32,128]{1,0:T(8,128)S(1)} %slice.29.refs_2_.refs_3_.refs_1_, ...), custom_call_target="tpu_custom_call" | custom-call | tf_op jit(solution)/shard_map/pallas_call | solution.py:192
  89.0 3.1 %shard_map.136 = (bf16[2048,2048]{1,0:T(8,128)(2,1)}, bf16[2048,2048]{1,0:T(8,128)(2,1)}, f32[2048]{0:T(1024)}, f32[2048]{0:T(1024)}) custom-call(bf16[12480,128]{1,0:T(8,128)(2,1)S(1)} %pack.22.refs_0_, bf16[12480,128]{1,0:T(8,128)(2,1)S(1)} %collective-permute-done.27.refs_1_, ...), custom_call_target="tpu_custom_call", output_to_operand_aliasing={{0}: (5, {}), {1}: (6, {})} | custom-call | tf_op jit(solution)/shard_map/pallas_call | solution.py:192
  92.1 1.9 %shard_map.137 = (bf16[2048,2048]{1,0:T(8,128)(2,1)}, bf16[2048,2048]{1,0:T(8,128)(2,1)}) custom-call(bf16[6240,128]{1,0:T(8,128)(2,1)S(1)} %pack.21.refs_0_, bf16[6240,128]{1,0:T(8,128)(2,1)S(1)} %collective-permute-done.26.refs_1_, f32[32,128]{1,0:T(8,128)S(1)} %slice.29.refs_2_.refs_3_.refs_1_, ...), custom_call_target="tpu_custom_call", output_to_operand_aliasing={{0}: (3, {}), {1}: (4, {})} | custom-call | tf_op jit(solution)/shard_map/pallas_call | solution.py:192
  (64 shorter events, 14.3 us)
Async XLA Ops:
  2.9 11.5 %collective-permute-start = (bf16[2080,128]{1,0:T(8,128)(2,1)S(1)}, bf16[2080,128]{1,0:T(8,128)(2,1)S(1)}, u32[]{:S(2)}, u32[]{:S(2)}) collective-permute-start(bf16[2080,128]{1,0:T(8,128)(2,1)S(1)} %get-tuple-element.28.refs_0_.refs_3_), channel_id=1, source_target_pairs={{0,8},{4,36},{8,16},{12,44},{16,24},{20,52},{24,0},{28,60},{32,40}... | collective-permute-start | bytes 1597448 | tf_op jit(solution)/shard_map/ppermute | solution.py:59
  5.4 9.0 %collective-permute-start.2 = (bf16[2080,128]{1,0:T(8,128)(2,1)S(1)}, bf16[2080,128]{1,0:T(8,128)(2,1)S(1)}, u32[]{:S(2)}, u32[]{:S(2)}) collective-permute-start(bf16[2080,128]{1,0:T(8,128)(2,1)S(1)} %get-tuple-element.28.refs_0_.refs_3_), channel_id=1, source_target_pairs={{0,24},{4,100},{8,0},{12,108},{16,8},{20,116},{24,16},{28,124},{32... | collective-permute-start | bytes 1597448 | tf_op jit(solution)/shard_map/ppermute | solution.py:59
  14.5 21.2 %collective-permute-start.19 = (bf16[4160,128]{1,0:T(8,128)(2,1)S(1)}, bf16[4160,128]{1,0:T(8,128)(2,1)S(1)}, u32[]{:S(2)}, u32[]{:S(2)}) collective-permute-start(bf16[4160,128]{1,0:T(8,128)(2,1)S(1)} %pack.18), channel_id=1, source_target_pairs={{0,32},{4,12},{8,40},{12,20},{16,48},{20,28},{24,56},{28,4},{32,64... | collective-permute-start | bytes 3194888 | tf_op jit(solution)/shard_map/ppermute | solution.py:63
  15.6 20.1 %collective-permute-start.23 = (bf16[4160,128]{1,0:T(8,128)(2,1)S(1)}, bf16[4160,128]{1,0:T(8,128)(2,1)S(1)}, u32[]{:S(2)}, u32[]{:S(2)}) collective-permute-start(bf16[4160,128]{1,0:T(8,128)(2,1)S(1)} %pack.18), channel_id=1, source_target_pairs={{0,96},{4,28},{8,104},{12,4},{16,112},{20,12},{24,120},{28,20},{32... | collective-permute-start | bytes 3194888 | tf_op jit(solution)/shard_map/ppermute | solution.py:63
  17.4 18.3 %collective-permute-start.18 = (bf16[2080,128]{1,0:T(8,128)(2,1)S(1)}, bf16[2080,128]{1,0:T(8,128)(2,1)S(1)}, u32[]{:S(2)}, u32[]{:S(2)}) collective-permute-start(bf16[2080,128]{1,0:T(8,128)(2,1)S(1)} %get-tuple-element.28.refs_0_.refs_3_), channel_id=1, source_target_pairs={{0,32},{4,12},{8,40},{12,20},{16,48},{20,28},{24,56},{28,4},{32,64... | collective-permute-start | bytes 1597448 | tf_op jit(solution)/shard_map/ppermute | solution.py:63
  17.5 18.3 %collective-permute-start.22 = (bf16[2080,128]{1,0:T(8,128)(2,1)S(1)}, bf16[2080,128]{1,0:T(8,128)(2,1)S(1)}, u32[]{:S(2)}, u32[]{:S(2)}) collective-permute-start(bf16[2080,128]{1,0:T(8,128)(2,1)S(1)} %get-tuple-element.28.refs_0_.refs_3_), channel_id=1, source_target_pairs={{0,96},{4,28},{8,104},{12,4},{16,112},{20,12},{24,120},{28,20},{32... | collective-permute-start | bytes 1597448 | tf_op jit(solution)/shard_map/ppermute | solution.py:63
  36.0 53.0 %collective-permute-start.27 = (bf16[12480,128]{1,0:T(8,128)(2,1)S(1)}, bf16[12480,128]{1,0:T(8,128)(2,1)S(1)}, u32[]{:S(2)}, u32[]{:S(2)}) collective-permute-start(bf16[12480,128]{1,0:T(8,128)(2,1)S(1)} %pack.22.refs_0_), channel_id=1, source_target_pairs={{0,4},{4,0},{1,5},{5,1},{2,6},{6,2},{3,7},{7,3},{8,12},{12,8},{9,1... | collective-permute-start | bytes 9584648 | tf_op jit(solution)/shard_map/ppermute | solution.py:67
  38.5 7.2 %collective-permute-start.1 = (bf16[1040,128]{1,0:T(8,128)(2,1)S(1)}, bf16[1040,128]{1,0:T(8,128)(2,1)S(1)}, u32[]{:S(2)}, u32[]{:S(2)}) collective-permute-start(bf16[1040,128]{1,0:T(8,128)(2,1)S(1)} %pack.12), channel_id=1, source_target_pairs={{0,8},{4,36},{8,16},{12,44},{16,24},{20,52},{24,0},{28,60},{32,40}... | collective-permute-start | bytes 798728 | tf_op jit(solution)/shard_map/ppermute | solution.py:59
  40.1 6.6 %collective-permute-start.3 = (bf16[1040,128]{1,0:T(8,128)(2,1)S(1)}, bf16[1040,128]{1,0:T(8,128)(2,1)S(1)}, u32[]{:S(2)}, u32[]{:S(2)}) collective-permute-start(bf16[1040,128]{1,0:T(8,128)(2,1)S(1)} %pack.13), channel_id=1, source_target_pairs={{0,24},{4,100},{8,0},{12,108},{16,8},{20,116},{24,16},{28,124},{32... | collective-permute-start | bytes 798728 | tf_op jit(solution)/shard_map/ppermute | solution.py:59
  41.7 6.1 %collective-permute-start.10 = (f32[48,128]{1,0:T(8,128)S(1)}, f32[48,128]{1,0:T(8,128)S(1)}, u32[]{:S(2)}, u32[]{:S(2)}) collective-permute-start(f32[48,128]{1,0:T(8,128)S(1)} %get-tuple-element.29), channel_id=1, source_target_pairs={{0,96},{4,28},{8,104},{12,4},{16,112},{20,12},{24,120},{28,20},{32... | collective-permute-start | bytes 73736 | tf_op jit(solution)/shard_map/ppermute | solution.py:63
  44.3 5.2 %collective-permute-start.11 = (f32[48,128]{1,0:T(8,128)S(1)}, f32[48,128]{1,0:T(8,128)S(1)}, u32[]{:S(2)}, u32[]{:S(2)}) collective-permute-start(f32[48,128]{1,0:T(8,128)S(1)} %get-tuple-element.29), channel_id=1, source_target_pairs={{0,64},{4,20},{8,72},{12,28},{16,80},{20,4},{24,88},{28,12},{32,96... | collective-permute-start | bytes 73736 | tf_op jit(solution)/shard_map/ppermute | solution.py:63
  45.7 4.2 %collective-permute-start.9 = (f32[48,128]{1,0:T(8,128)S(1)}, f32[48,128]{1,0:T(8,128)S(1)}, u32[]{:S(2)}, u32[]{:S(2)}) collective-permute-start(f32[48,128]{1,0:T(8,128)S(1)} %get-tuple-element.29), channel_id=1, source_target_pairs={{0,32},{4,12},{8,40},{12,20},{16,48},{20,28},{24,56},{28,4},{32,64... | collective-permute-start | bytes 73736 | tf_op jit(solution)/shard_map/ppermute | solution.py:63
  46.7 10.5 %collective-permute-start.4 = (bf16[2080,128]{1,0:T(8,128)(2,1)S(1)}, bf16[2080,128]{1,0:T(8,128)(2,1)S(1)}, u32[]{:S(2)}, u32[]{:S(2)}) collective-permute-start(bf16[2080,128]{1,0:T(8,128)(2,1)S(1)} %pack.14.refs_0_), channel_id=1, source_target_pairs={{0,32},{4,12},{8,40},{12,20},{16,48},{20,28},{24,56},{28,4},{32,64... | collective-permute-start | bytes 1597448 | tf_op jit(solution)/shard_map/ppermute | solution.py:63
  47.8 12.1 %collective-permute-start.6 = (bf16[2080,128]{1,0:T(8,128)(2,1)S(1)}, bf16[2080,128]{1,0:T(8,128)(2,1)S(1)}, u32[]{:S(2)}, u32[]{:S(2)}) collective-permute-start(bf16[2080,128]{1,0:T(8,128)(2,1)S(1)} %pack.14.refs_0_), channel_id=1, source_target_pairs={{0,96},{4,28},{8,104},{12,4},{16,112},{20,12},{24,120},{28,20},{32... | collective-permute-start | bytes 1597448 | tf_op jit(solution)/shard_map/ppermute | solution.py:63
  51.3 34.8 %collective-permute-start.28 = (bf16[6240,128]{1,0:T(8,128)(2,1)S(1)}, bf16[6240,128]{1,0:T(8,128)(2,1)S(1)}, u32[]{:S(2)}, u32[]{:S(2)}) collective-permute-start(bf16[6240,128]{1,0:T(8,128)(2,1)S(1)} %pack.23.refs_0_), channel_id=1, source_target_pairs={{0,4},{4,0},{1,5},{5,1},{2,6},{6,2},{3,7},{7,3},{8,12},{12,8},{9,1... | collective-permute-start | bytes 4792328 | tf_op jit(solution)/shard_map/ppermute | solution.py:67
  61.0 9.2 %collective-permute-start.5 = (bf16[1040,128]{1,0:T(8,128)(2,1)S(1)}, bf16[1040,128]{1,0:T(8,128)(2,1)S(1)}, u32[]{:S(2)}, u32[]{:S(2)}) collective-permute-start(bf16[1040,128]{1,0:T(8,128)(2,1)S(1)} %pack.15), channel_id=1, source_target_pairs={{0,32},{4,12},{8,40},{12,20},{16,48},{20,28},{24,56},{28,4},{32,64... | collective-permute-start | bytes 798728 | tf_op jit(solution)/shard_map/ppermute | solution.py:63
  61.1 9.2 %collective-permute-start.7 = (bf16[1040,128]{1,0:T(8,128)(2,1)S(1)}, bf16[1040,128]{1,0:T(8,128)(2,1)S(1)}, u32[]{:S(2)}, u32[]{:S(2)}) collective-permute-start(bf16[1040,128]{1,0:T(8,128)(2,1)S(1)} %pack.16), channel_id=1, source_target_pairs={{0,96},{4,28},{8,104},{12,4},{16,112},{20,12},{24,120},{28,20},{32... | collective-permute-start | bytes 798728 | tf_op jit(solution)/shard_map/ppermute | solution.py:63
  64.0 5.7 %collective-permute-start.17 = (f32[48,128]{1,0:T(8,128)S(1)}, f32[48,128]{1,0:T(8,128)S(1)}, u32[]{:S(2)}, u32[]{:S(2)}) collective-permute-start(f32[48,128]{1,0:T(8,128)S(1)} %add_add_fusion), channel_id=1, source_target_pairs={{0,4},{4,0},{1,5},{5,1},{2,6},{6,2},{3,7},{7,3},{8,12},{12,8},{9,1... | collective-permute-start | bytes 73736 | tf_op jit(solution)/shard_map/ppermute | solution.py:67
  69.8 22.3 %collective-permute-start.26 = (bf16[6240,128]{1,0:T(8,128)(2,1)S(1)}, bf16[6240,128]{1,0:T(8,128)(2,1)S(1)}, u32[]{:S(2)}, u32[]{:S(2)}) collective-permute-start(bf16[6240,128]{1,0:T(8,128)(2,1)S(1)} %pack.21.refs_0_), channel_id=1, source_target_pairs={{0,4},{4,0},{1,5},{5,1},{2,6},{6,2},{3,7},{7,3},{8,12},{12,8},{9,1... | collective-permute-start | bytes 4792328 | tf_op jit(solution)/shard_map/ppermute | solution.py:67
  70.2 12.5 %collective-permute-start.20 = (bf16[3120,128]{1,0:T(8,128)(2,1)S(1)}, bf16[3120,128]{1,0:T(8,128)(2,1)S(1)}, u32[]{:S(2)}, u32[]{:S(2)}) collective-permute-start(bf16[3120,128]{1,0:T(8,128)(2,1)S(1)} %pack.19), channel_id=1, source_target_pairs={{0,32},{4,12},{8,40},{12,20},{16,48},{20,28},{24,56},{28,4},{32,64... | collective-permute-start | bytes 2396168 | tf_op jit(solution)/shard_map/ppermute | solution.py:63
  70.3 15.7 %collective-permute-start.24 = (bf16[3120,128]{1,0:T(8,128)(2,1)S(1)}, bf16[3120,128]{1,0:T(8,128)(2,1)S(1)}, u32[]{:S(2)}, u32[]{:S(2)}) collective-permute-start(bf16[3120,128]{1,0:T(8,128)(2,1)S(1)} %pack.20), channel_id=1, source_target_pairs={{0,96},{4,28},{8,104},{12,4},{16,112},{20,12},{24,120},{28,20},{32... | collective-permute-start | bytes 2396168 | tf_op jit(solution)/shard_map/ppermute | solution.py:63
  82.8 12.5 %collective-permute-start.21 = (bf16[3120,128]{1,0:T(8,128)(2,1)S(1)}, bf16[3120,128]{1,0:T(8,128)(2,1)S(1)}, u32[]{:S(2)}, u32[]{:S(2)}) collective-permute-start(bf16[3120,128]{1,0:T(8,128)(2,1)S(1)} %collective-permute-done.20.refs_0_), channel_id=1, source_target_pairs={{0,4},{4,0},{1,5},{5,1},{2,6},{6,2},{3,7},{7,3},{8,12},{12,8},{9,1... | collective-permute-start | bytes 2396168 | tf_op jit(solution)/shard_map/ppermute | solution.py:67
  86.0 9.3 %collective-permute-start.25 = (bf16[3120,128]{1,0:T(8,128)(2,1)S(1)}, bf16[3120,128]{1,0:T(8,128)(2,1)S(1)}, u32[]{:S(2)}, u32[]{:S(2)}) collective-permute-start(bf16[3120,128]{1,0:T(8,128)(2,1)S(1)} %collective-permute-done.24.refs_1_), channel_id=1, source_target_pairs={{0,4},{4,0},{1,5},{5,1},{2,6},{6,2},{3,7},{7,3},{8,12},{12,8},{9,1... | collective-permute-start | bytes 2396168 | tf_op jit(solution)/shard_map/ppermute | solution.py:67
  86.0 10.8 %collective-permute-start.8 = (bf16[2080,128]{1,0:T(8,128)(2,1)S(1)}, bf16[2080,128]{1,0:T(8,128)(2,1)S(1)}, u32[]{:S(2)}, u32[]{:S(2)}) collective-permute-start(bf16[2080,128]{1,0:T(8,128)(2,1)S(1)} %pack.17.refs_2_), channel_id=1, source_target_pairs={{0,4},{4,0},{1,5},{5,1},{2,6},{6,2},{3,7},{7,3},{8,12},{12,8},{9,1... | collective-permute-start | bytes 1597448 | tf_op jit(solution)/shard_map/ppermute | solution.py:67
  (5 other events, 19.3 us)
